TPU v7x, 32 devices: a whole 2x2x4 slice. The times are simulated.
32 devices in a mesh: dp: 8 (over y, x, core), tensor: 4 (over z).
Axes of the slice: x: 2, y: 2, z: 4, core: 2. Of those that a mesh axis runs over, the one named last changes fastest.
Arguments:
- tokens: bfloat16 [16384, 768], P(('dp', 'tensor')), may hold values from -6 to 6
- segments: int32 [16384], P('dp'), may hold values from -1 to 9, as said below
- cotangent: bfloat16 [16384, 768], P(('dp', 'tensor')), may hold values from -6 to 6
- ln1_gain: bfloat16 [768], replicated, may hold values from 0.5 to 1.5
- ln1_bias: bfloat16 [768], replicated, may hold values from -2 to 2
- w_qkv: bfloat16 [768, 2304], P(None, 'tensor'), may hold values from -0.21875 to 0.21875
- q_bias: bfloat16 [768], P('tensor'), may hold values from -3 to 3
- v_bias: bfloat16 [768], P('tensor'), may hold values from -3 to 3
- w_out: bfloat16 [768, 768], P('tensor'), may hold values from -0.625 to 0.625
- out_bias: bfloat16 [768], replicated, may hold values from -2 to 2
- ln2_gain: bfloat16 [768], replicated, may hold values from 0.5 to 1.5
- ln2_bias: bfloat16 [768], replicated, may hold values from -2 to 2
- w_fc1: bfloat16 [768, 3072], P(None, 'tensor'), may hold values from -0.21875 to 0.21875
- fc1_bias: bfloat16 [3072], P('tensor'), may hold values from -3 to 3
- w_fc2: bfloat16 [3072, 768], P('tensor'), may hold values from -0.109375 to 0.109375
- fc2_bias: bfloat16 [768], replicated, may hold values from -2 to 2
Outputs:
- output: bfloat16 [16384, 768], P(('dp', 'tensor'))
- grad_tokens: bfloat16 [16384, 768], P(('dp', 'tensor'))
- cls_features: float32 [16384, 768], P(('dp', 'tensor'))
- grad_w_qkv: float32 [768, 2304], P('dp', 'tensor')
- grad_q_bias: float32 [768], replicated
- grad_v_bias: float32 [768], replicated
- grad_w_out: float32 [768, 768], P('tensor', 'dp')
- grad_out_bias: float32 [768], replicated
- grad_w_fc1: float32 [768, 3072], P('dp', 'tensor')
- grad_fc1_bias: float32 [3072], replicated
- grad_w_fc2: float32 [3072, 768], P('tensor', 'dp')
- grad_fc2_bias: float32 [768], replicated
- grad_ln1_gain: float32 [768], replicated
- grad_ln1_bias: float32 [768], replicated
- grad_ln2_gain: float32 [768], replicated
- grad_ln2_bias: float32 [768], replicated
Inputs may be any that keep to these rules, and one draw needn't show every extreme that they name: `segments`: within each aligned block of 512 positions the ids run 0, 1, 2, ... in order, id i over a run of 1 + 49 v positions with v from 1 to 4, starting at the block's first position; positions after the block's last whole sample hold -1. The first block begins with a run of 197; the last block holds only runs of 50, as many as fit.
All inputs are finite; a program needn't handle non-finite values.
Results may differ from a plain program's by a relative error of at most 0.024.
Values may be sent and summed in bfloat16 or wider, within the bound.
A program may use at most 128 MiB of HBM per device.

v0:
```python
from functools import partial
import math
import jax
import jax.numpy as jnp
from jax import lax
from jax.sharding import PartitionSpec as P

HD = 64
SEQ = 512


def layer_norm(values, gain, shift):
    average = jnp.mean(values, axis=-1, keepdims=True)
    centered = values - average
    spread = jnp.mean(centered * centered, axis=-1, keepdims=True)
    return centered * lax.rsqrt(spread + 1e-06) * gain + shift


def gelu_exact(values):
    return jax.nn.gelu(values, approximate=False)


def masked_scores(query_rows, key_rows, labels, score_scale):
    scores = (
        jnp.einsum("qhd,khd->hqk", query_rows, key_rows, preferred_element_type=jnp.float32)
        * score_scale
    )
    same_sample = labels[:, None] == labels[None, :]
    return jnp.where(same_sample[None], scores, -1e30)


def block_forward(inputs, score_scale):
    query_rows, key_rows, value_rows, labels = inputs
    scores = masked_scores(query_rows, key_rows, labels, score_scale)
    highest = jnp.max(scores, axis=-1, keepdims=True)
    expon = jnp.exp(scores - highest)
    totals = jnp.sum(expon, axis=-1, keepdims=True)
    weights = (expon / totals).astype(jnp.bfloat16)
    attended = jnp.einsum(
        "hqk,khd->qhd", weights, value_rows, preferred_element_type=jnp.float32
    ).astype(jnp.bfloat16)
    return (attended, (highest + jnp.log(totals))[..., 0])


def block_backward(inputs, score_scale):
    query_rows, key_rows, value_rows, labels, log_totals, grad_heads = inputs
    scores = masked_scores(query_rows, key_rows, labels, score_scale)
    weights = jnp.exp(scores - log_totals[..., None])
    grad_values = jnp.einsum(
        "hqk,qhd->khd", weights.astype(jnp.bfloat16), grad_heads, preferred_element_type=jnp.float32
    ).astype(jnp.bfloat16)
    grad_weights = jnp.einsum(
        "qhd,khd->hqk", grad_heads, value_rows, preferred_element_type=jnp.float32
    )
    inner = jnp.sum(grad_weights * weights, axis=-1, keepdims=True)
    grad_scores = (weights * (grad_weights - inner)).astype(jnp.bfloat16)
    grad_queries = (
        jnp.einsum("hqk,khd->qhd", grad_scores, key_rows, preferred_element_type=jnp.float32)
        * score_scale
    ).astype(jnp.bfloat16)
    grad_keys = (
        jnp.einsum("hqk,qhd->khd", grad_scores, query_rows, preferred_element_type=jnp.float32)
        * score_scale
    ).astype(jnp.bfloat16)
    return (grad_queries, grad_keys, grad_values)


def place_block(piece, tensor_index, tensor_parts):
    whole = jnp.zeros((piece.shape[0] * tensor_parts,), jnp.float32)
    return lax.dynamic_update_slice_in_dim(whole, piece, tensor_index * piece.shape[0], 0)


def on_device(
    tokens,
    segments,
    cotangent,
    ln1_gain,
    ln1_bias,
    w_qkv,
    q_bias,
    v_bias,
    w_out,
    out_bias,
    ln2_gain,
    ln2_bias,
    w_fc1,
    fc1_bias,
    w_fc2,
    fc2_bias,
):
    tensor_parts = lax.axis_size("tensor")
    tensor_index = lax.axis_index("tensor")
    rows_here = tokens.shape[0]
    all_rows = segments.shape[0]
    score_scale = 1.0 / math.sqrt(HD)
    positions = jnp.arange(all_rows) % SEQ
    earlier = jnp.concatenate([jnp.full((1,), -2, jnp.int32), segments[:-1]])
    first_all = ((segments >= 0) & ((positions == 0) | (segments != earlier))).astype(jnp.float32)
    first_rows = lax.dynamic_slice_in_dim(first_all, tensor_index * rows_here, rows_here)
    labels_here = lax.dynamic_slice_in_dim(segments, tensor_index * rows_here, rows_here)
    live_rows = (labels_here >= 0).astype(jnp.float32)
    inputs_f = tokens.astype(jnp.float32)
    normed, norm1_back = jax.vjp(
        layer_norm, inputs_f, ln1_gain.astype(jnp.float32), ln1_bias.astype(jnp.float32)
    )
    normed_low = normed.astype(jnp.bfloat16)
    weight_qkv, weight_out, bias_query, bias_value = (w_qkv, w_out, q_bias, v_bias)
    attn_source = lax.all_gather(normed_low, "tensor", axis=0, tiled=True)
    attn_total = attn_source.shape[0]
    block_count = attn_total // SEQ
    head_count = weight_qkv.shape[1] // (3 * HD)
    label_blocks = segments.reshape(block_count, SEQ)
    mixed = jnp.dot(attn_source, weight_qkv, preferred_element_type=jnp.float32).reshape(
        attn_total, head_count, 3, HD
    )
    query_rows = (mixed[:, :, 0] + bias_query.astype(jnp.float32).reshape(head_count, HD)).astype(
        jnp.bfloat16
    )
    key_rows = mixed[:, :, 1].astype(jnp.bfloat16)
    value_rows = (mixed[:, :, 2] + bias_value.astype(jnp.float32).reshape(head_count, HD)).astype(
        jnp.bfloat16
    )

    def blocked(array):
        return array.reshape(block_count, SEQ, head_count, HD)

    attended, log_totals = lax.map(
        partial(block_forward, score_scale=score_scale),
        (blocked(query_rows), blocked(key_rows), blocked(value_rows), label_blocks),
    )
    heads_out = attended.reshape(attn_total, head_count * HD)
    attn_sum = lax.psum_scatter(
        jnp.dot(heads_out, weight_out, preferred_element_type=jnp.float32).astype(jnp.bfloat16),
        "tensor",
        scatter_dimension=0,
        tiled=True,
    ).astype(jnp.float32)
    resid = inputs_f + attn_sum + out_bias.astype(jnp.float32)
    normed_two, norm2_back = jax.vjp(
        layer_norm, resid, ln2_gain.astype(jnp.float32), ln2_bias.astype(jnp.float32)
    )
    normed_two_low = normed_two.astype(jnp.bfloat16)
    gathered_two = lax.all_gather(normed_two_low, "tensor", axis=0, tiled=True)
    hidden = jnp.dot(gathered_two, w_fc1, preferred_element_type=jnp.float32) + fc1_bias.astype(
        jnp.float32
    )
    active, gelu_back = jax.vjp(gelu_exact, hidden)
    active_low = active.astype(jnp.bfloat16)
    branch = lax.psum_scatter(
        jnp.dot(active_low, w_fc2, preferred_element_type=jnp.float32).astype(jnp.bfloat16),
        "tensor",
        scatter_dimension=0,
        tiled=True,
    ).astype(jnp.float32)
    output_f = resid + branch + fc2_bias.astype(jnp.float32)
    output = output_f.astype(jnp.bfloat16)
    out_values = output.astype(jnp.float32)
    first_col = first_rows[:, None]
    moment_one, moment_two, cls_count = lax.psum(
        (
            jnp.sum(first_col * out_values, axis=0),
            jnp.sum(first_col * out_values * out_values, axis=0),
            jnp.sum(first_rows),
        ),
        ("dp", "tensor"),
    )
    cls_mean = moment_one / cls_count
    cls_spread = moment_two / cls_count - cls_mean * cls_mean
    cls_features = first_col * (out_values - cls_mean) * lax.rsqrt(cls_spread + 1e-05)
    grad_out = cotangent.astype(jnp.float32) * live_rows[:, None]
    grad_fc2_bias = jnp.sum(grad_out, axis=0)
    grad_branch = grad_out.astype(jnp.bfloat16)
    grad_rows = lax.all_gather(grad_branch, "tensor", axis=0, tiled=True)
    grad_fc2 = jnp.einsum("ni,nj->ij", active_low, grad_rows, preferred_element_type=jnp.float32)
    grad_active = jnp.dot(grad_rows, w_fc2.T, preferred_element_type=jnp.float32)
    grad_hidden = gelu_back(grad_active)[0].astype(jnp.bfloat16)
    grad_fc1 = jnp.einsum(
        "ni,nj->ij", gathered_two, grad_hidden, preferred_element_type=jnp.float32
    )
    grad_fc1_bias = place_block(
        jnp.sum(grad_hidden.astype(jnp.float32), axis=0), tensor_index, tensor_parts
    )
    grad_normed_two = lax.psum_scatter(
        jnp.dot(grad_hidden, w_fc1.T, preferred_element_type=jnp.float32).astype(jnp.bfloat16),
        "tensor",
        scatter_dimension=0,
        tiled=True,
    ).astype(jnp.float32)
    grad_resid_norm, grad_ln2_gain, grad_ln2_bias = norm2_back(grad_normed_two)
    grad_resid = grad_out + grad_resid_norm
    grad_out_bias = jnp.sum(grad_resid, axis=0)
    grad_attn = grad_resid.astype(jnp.bfloat16)
    attn_rows = lax.all_gather(grad_attn, "tensor", axis=0, tiled=True)
    grad_w_out = jnp.einsum("ni,nj->ij", heads_out, attn_rows, preferred_element_type=jnp.float32)
    grad_heads = jnp.dot(attn_rows, weight_out.T, preferred_element_type=jnp.float32).astype(
        jnp.bfloat16
    )
    grad_queries, grad_keys, grad_values = lax.map(
        partial(block_backward, score_scale=score_scale),
        (
            blocked(query_rows),
            blocked(key_rows),
            blocked(value_rows),
            label_blocks,
            log_totals,
            blocked(grad_heads),
        ),
    )
    grad_queries = grad_queries.reshape(attn_total, head_count, HD)
    grad_keys = grad_keys.reshape(attn_total, head_count, HD)
    grad_values = grad_values.reshape(attn_total, head_count, HD)
    grad_mixed = jnp.stack([grad_queries, grad_keys, grad_values], axis=2).reshape(
        attn_total, head_count * 3 * HD
    )
    query_sums = jnp.sum(grad_queries.astype(jnp.float32), axis=0).reshape(-1)
    value_sums = jnp.sum(grad_values.astype(jnp.float32), axis=0).reshape(-1)
    grad_w_qkv = jnp.einsum(
        "ni,nj->ij", attn_source, grad_mixed, preferred_element_type=jnp.float32
    )
    grad_q_bias = place_block(query_sums, tensor_index, tensor_parts)
    grad_v_bias = place_block(value_sums, tensor_index, tensor_parts)
    grad_normed = lax.psum_scatter(
        jnp.dot(grad_mixed, weight_qkv.T, preferred_element_type=jnp.float32).astype(jnp.bfloat16),
        "tensor",
        scatter_dimension=0,
        tiled=True,
    ).astype(jnp.float32)
    grad_inputs_norm, grad_ln1_gain, grad_ln1_bias = norm1_back(grad_normed)
    grad_tokens = (grad_resid + grad_inputs_norm).astype(jnp.bfloat16)
    sum_qkv, sum_out, sum_fc1, sum_fc2 = (
        lax.psum_scatter(grad_w_qkv, "dp", scatter_dimension=0, tiled=True),
        lax.psum_scatter(grad_w_out, "dp", scatter_dimension=1, tiled=True),
        lax.psum_scatter(grad_fc1, "dp", scatter_dimension=0, tiled=True),
        lax.psum_scatter(grad_fc2, "dp", scatter_dimension=1, tiled=True),
    )
    small_sums = lax.psum(
        (
            grad_ln1_gain,
            grad_ln1_bias,
            grad_q_bias,
            grad_v_bias,
            grad_out_bias,
            grad_fc1_bias,
            grad_fc2_bias,
            grad_ln2_gain,
            grad_ln2_bias,
        ),
        ("dp", "tensor"),
    )
    return (
        output,
        grad_tokens,
        cls_features,
        sum_qkv,
        small_sums[2],
        small_sums[3],
        sum_out,
        small_sums[4],
        sum_fc1,
        small_sums[5],
        sum_fc2,
        small_sums[6],
        small_sums[0],
        small_sums[1],
        small_sums[7],
        small_sums[8],
    )


def solution(mesh):
    in_specs = (
        P(("dp", "tensor"), None),
        P("dp"),
        P(("dp", "tensor"), None),
        P(),
        P(),
        P(None, "tensor"),
        P("tensor"),
        P("tensor"),
        P("tensor", None),
        P(),
        P(),
        P(),
        P(None, "tensor"),
        P("tensor"),
        P("tensor", None),
        P(),
    )
    out_specs = (
        P(("dp", "tensor"), None),
        P(("dp", "tensor"), None),
        P(("dp", "tensor"), None),
        P("dp", "tensor"),
        P(),
        P(),
        P("tensor", "dp"),
        P(),
        P("dp", "tensor"),
        P(),
        P("tensor", "dp"),
        P(),
        P(),
        P(),
        P(),
        P(),
    )
    return jax.shard_map(
        on_device, mesh=mesh, in_specs=in_specs, out_specs=out_specs, check_vma=False
    )
```

profile of v0, /device:TPU:0, one launch (start us, length us, event | category | flops | bytes accessed | tf_op | source)
XLA Modules:
  0.0 796.6 jit_solution(3495754331182693921)
XLA Ops:
  12.2 2.4 fusion.70
  14.8 66.1 %all-gather.5.cloned.1.call-done = bf16[2048,768]{1,0:T(8,128)(2,1)} async-done(((bf16[512,768]{1,0:T(8,128)(2,1)}), bf16[2048,768]{1,0:T(8,128)(2,1)}) %all-gather.5.cloned.1.call-update) | async-done | bytes 3145744 | tf_op jit(solution)/shard_map/all_gather | solution.py:108
  80.9 3.9 fusion.97
  86.3 3.2 squeeze.35
  89.5 1.8 add_convert_fusion.5
  92.3 2.2 squeeze.36
  94.5 1.8 add_convert_fusion.4
  98.2 20.1 %while.26 = (s32[]{:T(128)}, bf16[4,512,3,64]{1,3,2,0:T(8,128)(2,1)}, f32[4,3,512]{2,1,0:T(4,128)}, bf16[4,512,3,64]{1,3,2,0:T(8,128)(2,1)}, s32[4,512]{1,0:T(4,...) while((s32[]{:T(128)}, ...), condition=%wide.region_5.6_spmd, body=%wide.region_2.5_spmd.sunk | while | flops 211122688 | bytes 11332185 | solution.py:127
  100.5 2.7 fusion.146
  105.5 2.7 fusion.146
  110.6 2.7 fusion.146
  115.6 2.7 fusion.146
  118.3 2.0 copy.66
  121.4 2.7 convolution_convert_fusion.3
  125.5 57.9 %reduce-scatter.11.cloned.1.call-done = bf16[512,768]{1,0:T(8,128)(2,1)} async-done(((bf16[2048,768]{1,0:T(8,128)(2,1)}), bf16[512,768]{1,0:T(8,128)(2,1)}) %reduce-scatter.11.cloned.1.call-update) | async-done | bytes 786448 | tf_op jit(solution)/shard_map/reduce_scatter | solution.py:132
  189.1 2.1 fusion.95
  191.8 2.2 fusion.81
  195.3 57.2 %all-gather.7.cloned.1.call-done = bf16[2048,768]{1,0:T(8,128)(2,1)} async-done(((bf16[512,768]{1,0:T(8,128)(2,1)}), bf16[2048,768]{1,0:T(8,128)(2,1)}) %all-gather.7.cloned.1.call-update) | async-done | bytes 3145744 | tf_op jit(solution)/shard_map/all_gather | solution.py:143
  252.5 7.5 fusion.98
  260.0 56.6 %all-gather.9.cloned.1.call-done = bf16[2048,768]{1,0:T(8,128)(2,1)} async-done(((bf16[512,768]{1,0:T(8,128)(2,1)}), bf16[2048,768]{1,0:T(8,128)(2,1)}) %all-gather.9.cloned.1.call-update) | async-done | bytes 3145744 | tf_op jit(solution)/shard_map/all_gather | solution.py:173
  316.6 20.2 %convert_reduce_fusion = (f32[768]{0:T(1024)}, bf16[2048,768]{1,0:T(8,128)(2,1)S(1)}, f32[2048,768]{1,0:T(8,128)}) fusion(f32[2048,768]{1,0:T(8,128)} %fusion.98, f32[768]{0:T(1024)} %convert_element_type.159, bf16[2048,768]{1,0:T(8,128)(2,1)} %all-gather.9.cloned.1.call-done, bf16[768,768]{1,0:T(8,128)(2,1)S(1)} %copy-done), kind=kOutput, calls=%fused_computation.64 | convolution fusion | flops 2533883136 | bytes 20060160 | tf_op jit(solution)/shard_map/dot_general | solution.py:175
  338.5 4.0 convolution_convert_fusion
  342.6 5.5 multiply_convert_fusion.1
  349.7 4.0 convolution_convert_fusion.1
  353.8 10.8 %all-gather.11.cloned.1.call-start = ((), (), s32[]{:S(2)}) async-start(), calls=%async_computation.14 | async-start | bytes 3932160 | tf_op jit(solution)/shard_map/all_gather | solution.py:193
  364.6 37.1 %reduce-scatter.15.cloned.1.call-done = bf16[512,768]{1,0:T(8,128)(2,1)} async-done(((bf16[2048,768]{1,0:T(8,128)(2,1)}), bf16[512,768]{1,0:T(8,128)(2,1)}) %reduce-scatter.15.cloned.1.call-update) | async-done | bytes 786448 | tf_op jit(solution)/shard_map/reduce_scatter | solution.py:183
  401.7 1.9 convert_reduce_fusion.2
  403.7 2.2 fusion.75
  405.9 58.3 %reduce-scatter.13.cloned.1.call-done = bf16[512,768]{1,0:T(8,128)(2,1)} async-done(((bf16[2048,768]{1,0:T(8,128)(2,1)}), bf16[512,768]{1,0:T(8,128)(2,1)}) %reduce-scatter.13.cloned.1.call-update) | async-done | bytes 786448 | tf_op jit(solution)/shard_map/reduce_scatter | solution.py:149
  464.2 3.4 fusion.94
  469.8 63.4 %all-gather.11.cloned.1.call-done = bf16[2048,768]{1,0:T(8,128)(2,1)} async-done(((bf16[512,768]{1,0:T(8,128)(2,1)}), bf16[2048,768]{1,0:T(8,128)(2,1)}) %all-gather.11.cloned.1.call-update) | async-done | bytes 3145744 | tf_op jit(solution)/shard_map/all_gather | solution.py:193
  533.2 4.2 convolution_bitcast_fusion
  537.5 3.1 convolution_convert_fusion.4
  546.2 31.7 %while.27 = (s32[]{:T(128)}, bf16[4,512,3,64]{1,3,2,0:T(8,128)(2,1)}, bf16[4,512,3,64]{1,3,2,0:T(8,128)(2,1)}, bf16[4,512,3,64]{1,3,2,0:T(8,128)(2,1)}, bf16[4,5...) while((s32[]{:T(128)}, ...), condition=%wide.region_15.16_spmd, body=%wide.region_13.15_spmd.sunk | while | flops 511146496 | bytes 26127476 | solution.py:198
  580.2 1.7 copy.73
  582.5 2.6 copy.71
  585.2 2.1 stack_reshape.9
  589.3 4.1 convolution_convert_fusion.2
  593.7 6.9 fusion.100
  600.7 6.9 fusion.101
  607.7 6.5 fusion.99
  619.5 33.0 %reduce-scatter.17.cloned.1.call-done = bf16[512,768]{1,0:T(8,128)(2,1)} async-done(((bf16[2048,768]{1,0:T(8,128)(2,1)}), bf16[512,768]{1,0:T(8,128)(2,1)}) %reduce-scatter.17.cloned.1.call-update) | async-done | bytes 786448 | tf_op jit(solution)/shard_map/reduce_scatter | solution.py:222
  654.3 2.1 fusion.76
  656.4 41.9 %all-reduce = (f32[768]{0:T(1024)S(1)}, f32[]{:T(128)}, f32[768]{0:T(1024)S(1)}, f32[768]{0:T(1024)}, f32[768]{0:T(1024)}, /*index=5*/f32[768]{0:T(1024)}, f32[3...) all-reduce(f32[768]{0:T(1024)S(1)} %get-tuple-element.228, ...), channel_id=1, replica_groups=mesh['dp'=8,'tensor'=4] {'dp','tensor'}, use_global_device_ids=true, to_apply=%region_24.25 | all-reduce | flops 10753 | bytes 86024 | tf_op jit(solution)/shard_map/psum | solution.py:159
  699.0 2.6 fusion.78
  701.6 2.6 add_convert_fusion.1
  704.2 41.2 %reduce-scatter.23.cloned.1.call-done = f32[768,96]{0,1:T(8,128)} async-done(((f32[768,768]{0,1:T(8,128)}), f32[768,96]{0,1:T(8,128)}) %reduce-scatter.23.cloned.1.call-update) | async-done | bytes 294928 | tf_op jit(solution)/shard_map/reduce_scatter | solution.py:234
  745.4 44.0 %reduce-scatter.19.cloned.1.call-done = f32[96,576]{1,0:T(8,128)} async-done(((f32[768,576]{1,0:T(8,128)}), f32[96,576]{1,0:T(8,128)}) %reduce-scatter.19.cloned.1.call-update) | async-done | bytes 221200 | tf_op jit(solution)/shard_map/reduce_scatter | solution.py:231
  (231 shorter events, 84.7 us)
Async XLA Ops:
  7.2 309.5 %copy-start = (bf16[768,768]{1,0:T(8,128)(2,1)S(1)}, bf16[768,768]{1,0:T(8,128)(2,1)}, u32[]{:S(2)}) copy-start(bf16[768,768]{1,0:T(8,128)(2,1)} %param.34) | copy-start | bytes 3538948
  7.2 7.5 copy-start.39
  7.2 7.5 copy-start.40
  7.2 7.6 copy-start.21
  7.2 73.7 %copy-start.42 = (bf16[768,576]{0,1:T(8,128)(2,1)S(1)}, bf16[768,576]{0,1:T(8,128)(2,1)}, u32[]{:S(2)}) copy-start(bf16[768,576]{0,1:T(8,128)(2,1)} %param.25) | copy-start | bytes 2654212
  7.2 73.7 %all-gather.5.cloned.1.call-start = ((), (), s32[]{:S(2)}) async-start(), calls=%async_computation.8 | async-start | bytes 3932160 | tf_op jit(solution)/shard_map/all_gather | solution.py:108
  8.7 76.1 %copy-start.17 = (f32[512]{0:T(512)}, f32[512]{0:T(512)S(1)}, u32[]{:S(2)}) copy-start(f32[512]{0:T(512)S(1)} %broadcast_multiply_fusion.1) | copy-start | bytes 6148
  10.8 74.0 %copy-start.22 = (f32[512]{0:T(512)}, f32[512]{0:T(512)S(1)}, u32[]{:S(2)}) copy-start(f32[512]{0:T(512)S(1)} %fusion.90) | copy-start | bytes 6148
  11.5 73.3 %copy-start.15 = (f32[768]{0:T(1024)}, f32[768]{0:T(1024)S(1)}, u32[]{:S(2)}) copy-start(f32[768]{0:T(1024)S(1)} %convert_element_type.147) | copy-start | bytes 9220
  14.6 168.8 %reduce-scatter.11.cloned.1.call-start = ((), (), s32[]{:S(2)}) async-start(), calls=%async_computation.9 | async-start | bytes 3932160 | tf_op jit(solution)/shard_map/reduce_scatter | solution.py:132
  118.3 5.8 copy-start.6
  118.3 3.1 copy-start.13
  124.1 59.3 %copy-start.2 = (bf16[512,768]{1,0:T(8,128)(2,1)S(1)}, bf16[512,768]{1,0:T(8,128)(2,1)}, u32[]{:S(2)}) copy-start(bf16[512,768]{1,0:T(8,128)(2,1)} %param.20) | copy-start | bytes 2359300
  124.1 128.4 %all-gather.7.cloned.1.call-start = ((), (), s32[]{:S(2)}) async-start(), calls=%async_computation.10 | async-start | bytes 3932160 | tf_op jit(solution)/shard_map/all_gather | solution.py:143
  183.3 4.3 copy-start.3
  183.3 4.3 copy-start.33
  184.9 2.2 copy-start.19
  189.0 127.6 %all-gather.9.cloned.1.call-start = ((), (), s32[]{:S(2)}) async-start(), calls=%async_computation.12 | async-start | bytes 3932160 | tf_op jit(solution)/shard_map/all_gather | solution.py:173
  194.0 207.7 %reduce-scatter.15.cloned.1.call-start = ((), (), s32[]{:S(2)}) async-start(), calls=%async_computation.13 | async-start | bytes 3932160 | tf_op jit(solution)/shard_map/reduce_scatter | solution.py:183
  316.6 21.8 %copy-start.41 = (bf16[768,768]{1,0:T(8,128)(2,1)S(1)}, bf16[768,768]{1,0:T(8,128)(2,1)}, u32[]{:S(2)}) copy-start(bf16[768,768]{1,0:T(8,128)(2,1)} %param.32) | copy-start | bytes 3538948
  336.8 1.6 copy-start.44
  342.5 121.7 %reduce-scatter.13.cloned.1.call-start = ((), (), s32[]{:S(2)}) async-start(), calls=%async_computation.11 | async-start | bytes 3932160 | tf_op jit(solution)/shard_map/reduce_scatter | solution.py:149
  348.1 1.7 copy-start.11
  353.7 10.9 %copy-start.38 = (bf16[768]{0:T(1024)(128)(2,1)S(1)}, bf16[768]{0:T(1024)(128)(2,1)}, u32[]{:S(2)}) copy-start(bf16[768]{0:T(1024)(128)(2,1)} %param.35) | copy-start | bytes 4612
  353.7 48.0 %copy-start.20 = (f32[512]{0:T(512)S(1)}, f32[512]{0:T(512)}, u32[]{:S(2)}) copy-start(f32[512]{0:T(512)} %copy-done.19) | copy-start | bytes 6148
  353.7 49.9 %copy-start.31 = (f32[512]{0:T(512)S(1)}, f32[512]{0:T(512)}, u32[]{:S(2)}) copy-start(f32[512]{0:T(512)} %copy-done.30) | copy-start | bytes 6148
  353.7 49.9 %copy-start.25 = (f32[512]{0:T(512)S(1)}, f32[512]{0:T(512)}, u32[]{:S(2)}) copy-start(f32[512]{0:T(512)} %copy-done.24) | copy-start | bytes 6148
  353.7 110.5 %copy-start.27 = (f32[512]{0:T(512)S(1)}, f32[512]{0:T(512)}, u32[]{:S(2)}) copy-start(f32[512]{0:T(512)} %copy-done.26) | copy-start | bytes 6148
  353.8 110.5 %copy-start.32 = (f32[512]{0:T(512)S(1)}, f32[512]{0:T(512)}, u32[]{:S(2)}) copy-start(f32[512]{0:T(512)} %get-tuple-element.219) | copy-start | bytes 6148
  353.8 179.5 %all-gather.11.cloned.1.call-start = ((), (), s32[]{:S(2)}) async-start(), calls=%async_computation.14 | async-start | bytes 3932160 | tf_op jit(solution)/shard_map/all_gather | solution.py:193
  401.7 62.5 %copy-start.8 = (bf16[512,768]{1,0:T(8,128)(2,1)S(1)}, bf16[512,768]{1,0:T(8,128)(2,1)}, u32[]{:S(2)}) copy-start(bf16[512,768]{1,0:T(8,128)(2,1)} %reduce-scatter.15.cloned.1.call-done) | copy-start | bytes 2359300
  467.6 65.6 %copy-start.10 = (bf16[24,8,4,512]{3,1,2,0:T(8,128)(2,1)S(1)}, bf16[24,8,4,512]{3,1,2,0:T(8,128)(2,1)}, u32[]{:S(2)}) copy-start(bf16[24,8,4,512]{3,1,2,0:T(8,128)(2,1)} %copy-done.9) | copy-start | bytes 2359300
  469.7 148.2 %reduce-scatter.25.cloned.1.call-start = ((), (), s32[]{:S(2)}) async-start(), calls=%async_computation.19 | async-start | bytes 884736
  469.8 67.7 %copy-start.14 = (bf16[192,768]{1,0:T(8,128)(2,1)S(1)}, bf16[192,768]{1,0:T(8,128)(2,1)}, u32[]{:S(2)}) copy-start(bf16[192,768]{1,0:T(8,128)(2,1)} %param.28) | copy-start | bytes 884740
  537.4 115.2 %reduce-scatter.17.cloned.1.call-start = ((), (), s32[]{:S(2)}) async-start(), calls=%async_computation.15 | async-start | bytes 3932160 | tf_op jit(solution)/shard_map/reduce_scatter | solution.py:222
  540.5 5.6 copy-start.7
  587.5 1.8 copy-start.43
  587.8 1.5 copy-start.12
  593.4 110.8 %reduce-scatter.21.cloned.1.call-start = ((), (), s32[]{:S(2)}) async-start(), calls=%async_computation.17 | async-start | bytes 2654208 | tf_op jit(solution)/shard_map/reduce_scatter | solution.py:233
  600.6 144.8 %reduce-scatter.23.cloned.1.call-start = ((), (), s32[]{:S(2)}) async-start(), calls=%async_computation.18 | async-start | bytes 2654208 | tf_op jit(solution)/shard_map/reduce_scatter | solution.py:234
  607.6 6.7 copy-start.34
  607.6 181.8 %reduce-scatter.19.cloned.1.call-start = ((), (), s32[]{:S(2)}) async-start(), calls=%async_computation.16 | async-start | bytes 2211840 | tf_op jit(solution)/shard_map/reduce_scatter | solution.py:231
  614.2 38.4 %copy-start.16 = (f32[768]{0:T(1024)S(1)}, f32[768]{0:T(1024)}, u32[]{:S(2)}) copy-start(f32[768]{0:T(1024)} %copy-done.15) | copy-start | bytes 9220
  614.2 38.4 %copy-start.18 = (f32[512]{0:T(512)S(1)}, f32[512]{0:T(512)}, u32[]{:S(2)}) copy-start(f32[512]{0:T(512)} %copy-done.17) | copy-start | bytes 6148
  614.2 40.1 %copy-start.29 = (f32[512]{0:T(512)S(1)}, f32[512]{0:T(512)}, u32[]{:S(2)}) copy-start(f32[512]{0:T(512)} %copy-done.28) | copy-start | bytes 6148
  614.2 40.1 %copy-start.23 = (f32[512]{0:T(512)S(1)}, f32[512]{0:T(512)}, u32[]{:S(2)}) copy-start(f32[512]{0:T(512)} %copy-done.22) | copy-start | bytes 6148
  616.0 85.6 %copy-start.5 = (f32[512,768]{1,0:T(8,128)S(1)}, f32[512,768]{1,0:T(8,128)}, u32[]{:S(2)}) copy-start(f32[512,768]{1,0:T(8,128)} %copy-done.4) | copy-start | bytes 4718596
  698.9 90.5 %copy-start.1 = (bf16[768,768]{1,0:T(8,128)(2,1)S(1)}, bf16[768,768]{1,0:T(8,128)(2,1)}, u32[]{:S(2)}) copy-start(bf16[768,768]{1,0:T(8,128)(2,1)} %param.34) | copy-start | bytes 3538948
  (9 other events, 6.5 us)
Sparse Core Ops, SparseCore 0:
  14.7 66.1 all-gather.4
  124.3 59.0 reduce-scatter.10
  189.1 63.3 all-gather.6
  254.5 62.0 all-gather.8
  342.6 59.0 reduce-scatter.14
  403.9 60.3 reduce-scatter.12
  469.8 63.3 all-gather.10
  537.5 33.5 reduce-scatter.24
  593.5 59.0 reduce-scatter.16
  656.4 42.6 reduce-scatter.20
  703.0 42.3 reduce-scatter.22
  749.2 40.1 reduce-scatter.18
where the time goes:
time: 806 us; the launch traced here: 797 us
  waiting for transfers between devices  515 us (64%)
  matrix products  112 us (14%)
  other arithmetic  57.9 us (7%)
  local copies, waits for them, and re-layouts  42.5 us (5%)
  blocking collectives  41.9 us (5%)
  between operations  15.1 us (2%)
  starting transfers between devices  11.8 us (1%)
    all_gather x1, waiting for transfers between devices, on_device(): attn_source = lax.all_gather(normed_low, 'tensor', axis=0, tiled=True)  66.1 us
    all_gather x1, waiting for transfers between devices, on_device(): attn_rows = lax.all_gather(grad_attn, 'tensor', axis=0, tiled=True)  63.4 us
    reduce_scatter x1, waiting for transfers between devices, on_device(): lax.psum_scatter(jnp.dot(active_low, w_fc2, preferred_element_type=jnp.fl...  58.3 us
    reduce_scatter x1, waiting for transfers between devices, on_device(): lax.psum_scatter(jnp.dot(heads_out, weight_out, preferred_element_type=jn...  57.9 us
    all_gather x1, waiting for transfers between devices, on_device(): gathered_two = lax.all_gather(normed_two_low, 'tensor', axis=0, tiled=True)  57.2 us
    all_gather x1, waiting for transfers between devices, on_device(): grad_rows = lax.all_gather(grad_branch, 'tensor', axis=0, tiled=True)  56.6 us
    reduce_scatter x1, waiting for transfers between devices, on_device(): lax.psum_scatter(grad_w_qkv, 'dp', scatter_dimension=0, tiled=True)  44 us
    psum x1, blocking collectives, on_device(): lax.psum((jnp.sum(first_col * out_values, axis=0), jnp.sum(first_col * ou...  41.9 us
  transfers between devices with their start and end apart: 12, of which 10 were waited for; matrix products, arithmetic and copies ran while one was open for 15% of the time, Pallas kernels for 0%

commit v1 on v0

--- a/solution.py
+++ b/solution.py
@@ -140,7 +140,30 @@
         layer_norm, resid, ln2_gain.astype(jnp.float32), ln2_bias.astype(jnp.float32)
     )
     normed_two_low = normed_two.astype(jnp.bfloat16)
-    gathered_two = lax.all_gather(normed_two_low, "tensor", axis=0, tiled=True)
+    now = lax.axis_size("tensor")
+    q_next = lax.axis_index("tensor")
+    arr_now, x_next, piece_now = (now, q_next, normed_two_low.shape[0])
+    table = [(p, (p + 1) % arr_now) for p in range(arr_now)]
+    lanes = [(p, (p - 1) % arr_now) for p in range(arr_now)]
+    gathered_two = jnp.zeros(
+        (*normed_two_low.shape[:0], arr_now * piece_now, *normed_two_low.shape[1:]),
+        normed_two_low.dtype,
+    )
+    gathered_two = lax.dynamic_update_slice_in_dim(
+        gathered_two, normed_two_low, x_next * piece_now, axis=0
+    )
+    e_next = vec_out = normed_two_low
+    a_now = arr_now // 2
+    for nth in range(1, a_now + 1):
+        e_next = lax.ppermute(e_next, "tensor", perm=table)
+        gathered_two = lax.dynamic_update_slice_in_dim(
+            gathered_two, e_next, (x_next - nth) % arr_now * piece_now, axis=0
+        )
+        if nth < arr_now - a_now:
+            vec_out = lax.ppermute(vec_out, "tensor", lanes)
+            gathered_two = lax.dynamic_update_slice_in_dim(
+                gathered_two, vec_out, (x_next + nth) % arr_now * piece_now, axis=0
+            )
     hidden = jnp.dot(gathered_two, w_fc1, preferred_element_type=jnp.float32) + fc1_bias.astype(
         jnp.float32
     )

time: 806 us -> 795 us (0.986)
  waiting for transfers between devices: 515 us -> 460 us
  starting transfers between devices: 11.8 us -> 47.4 us
    ppermute x0 -> x3, waiting for transfers between devices: none -> 62.5 us  [the longest x2 62.4 us: on_device(): e_next = lax.ppermute(e_next, 'tensor', perm=table)]
    all_gather x1 -> x0, waiting for transfers between devices: 57.2 us -> none  [on_device(): gathered_two = lax.all_gather(normed_two_low, 'tensor', axis=0, tiled=True)]
    all_gather x1, waiting for transfers between devices: 56.6 us -> 0.01 us  [on_device(): grad_rows = lax.all_gather(grad_branch, 'tensor', axis=0, tiled=True)]
    ppermute x0 -> x3, starting transfers between devices: none -> 35.7 us  [the longest x2 32.7 us: on_device(): e_next = lax.ppermute(e_next, 'tensor', perm=table)]
  transfers between devices with their start and end apart: 12 -> 14, of which waited for: 10 -> 10; matrix products, arithmetic and copies ran while one was open for 15% -> 17% of each run, Pallas kernels for 0% -> 0%
where the time goes in v1:
time: 795 us; the launch traced here: 785 us
  waiting for transfers between devices  460 us (58%)
  matrix products  112 us (14%)
  other arithmetic  58.4 us (7%)
  local copies, waits for them, and re-layouts  50.4 us (6%)
  starting transfers between devices  47.4 us (6%)
  blocking collectives  41.8 us (5%)
  between operations  14.8 us (2%)
    all_gather x1, waiting for transfers between devices, on_device(): attn_source = lax.all_gather(normed_low, 'tensor', axis=0, tiled=True)  64.9 us
    all_gather x1, waiting for transfers between devices, on_device(): attn_rows = lax.all_gather(grad_attn, 'tensor', axis=0, tiled=True)  63.4 us
    ppermute x2, waiting for transfers between devices, on_device(): e_next = lax.ppermute(e_next, 'tensor', perm=table)  62.4 us
    reduce_scatter x1, waiting for transfers between devices, on_device(): lax.psum_scatter(jnp.dot(active_low, w_fc2, preferred_element_type=jnp.fl...  58.3 us
    reduce_scatter x1, waiting for transfers between devices, on_device(): lax.psum_scatter(jnp.dot(heads_out, weight_out, preferred_element_type=jn...  53.7 us
    reduce_scatter x1, waiting for transfers between devices, on_device(): lax.psum_scatter(grad_w_qkv, 'dp', scatter_dimension=0, tiled=True)  44.2 us
    psum x1, blocking collectives, on_device(): lax.psum((jnp.sum(first_col * out_values, axis=0), jnp.sum(first_col * ou...  41.8 us
    reduce_scatter x1, waiting for transfers between devices, on_device(): lax.psum_scatter(grad_fc2, 'dp', scatter_dimension=1, tiled=True)  41.2 us
  transfers between devices with their start and end apart: 14, of which 10 were waited for; matrix products, arithmetic and copies ran while one was open for 17% of the time, Pallas kernels for 0%

profile of v1, /device:TPU:0, one launch (start us, length us, event | category | flops | bytes accessed | tf_op | source)
XLA Modules:
  0.0 784.9 jit_solution(18319248191558617697)
XLA Ops:
  12.2 2.4 fusion.70
  16.0 64.9 %all-gather.4.cloned.1.call-done = bf16[2048,768]{1,0:T(8,128)(2,1)} async-done(((bf16[512,768]{1,0:T(8,128)(2,1)}), bf16[2048,768]{1,0:T(8,128)(2,1)}) %all-gather.4.cloned.1.call-update) | async-done | bytes 3145744 | tf_op jit(solution)/shard_map/all_gather | solution.py:108
  80.9 3.9 fusion.97
  86.3 3.2 squeeze.35
  92.3 2.2 squeeze.36
  98.2 20.1 %while.26 = (s32[]{:T(128)}, bf16[4,512,3,64]{1,3,2,0:T(8,128)(2,1)}, f32[4,3,512]{2,1,0:T(4,128)}, bf16[4,512,3,64]{1,3,2,0:T(8,128)(2,1)}, s32[4,512]{1,0:T(4,...) while((s32[]{:T(128)}, ...), condition=%wide.region_5.6_spmd, body=%wide.region_2.5_spmd.sunk | while | flops 211122688 | bytes 11332185 | solution.py:127
  100.5 2.7 fusion.146
  105.5 2.7 fusion.146
  110.6 2.7 fusion.146
  115.6 2.7 fusion.146
  118.3 2.0 copy.66
  121.4 2.7 convolution_convert_fusion.3
  129.6 53.7 %reduce-scatter.11.cloned.1.call-done = bf16[512,768]{1,0:T(8,128)(2,1)} async-done(((bf16[2048,768]{1,0:T(8,128)(2,1)}), bf16[512,768]{1,0:T(8,128)(2,1)}) %reduce-scatter.11.cloned.1.call-update) | async-done | bytes 786448 | tf_op jit(solution)/shard_map/reduce_scatter | solution.py:132
  187.1 2.0 broadcast_in_dim.82
  191.5 3.0 collective-permute-start.1
  194.5 33.9 %collective-permute-done = bf16[512,768]{1,0:T(8,128)(2,1)} collective-permute-done((bf16[512,768]{1,0:T(8,128)(2,1)}, bf16[512,768]{1,0:T(8,128)(2,1)}, u32[]{:S(2)}, u32[]{:S(2)}) %collective-permute-start) | collective-permute-done | bytes 786464 | tf_op jit(solution)/shard_map/ppermute | solution.py:158
  228.5 31.8 %collective-permute-start.2 = (bf16[512,768]{1,0:T(8,128)(2,1)}, bf16[512,768]{1,0:T(8,128)(2,1)}, u32[]{:S(2)}, u32[]{:S(2)}) collective-permute-start(bf16[512,768]{1,0:T(8,128)(2,1)} %collective-permute-done), channel_id=1, source_target_pairs={{0,1},{1,2},{2,3},{3,0},{4,5},{5,6},{6,7},{7,4},{8,9},{9,10},{10,1... | collective-permute-start | bytes 2359304 | tf_op jit(solution)/shard_map/ppermute | solution.py:158
  261.6 2.2 constant_dynamic-update-slice_fusion.2
  263.8 2.1 constant_dynamic-update-slice_fusion.1
  265.8 28.5 %collective-permute-done.2 = bf16[512,768]{1,0:T(8,128)(2,1)} collective-permute-done((bf16[512,768]{1,0:T(8,128)(2,1)}, bf16[512,768]{1,0:T(8,128)(2,1)}, u32[]{:S(2)}, u32[]{:S(2)}) %collective-permute-start.2) | collective-permute-done | bytes 786464 | tf_op jit(solution)/shard_map/ppermute | solution.py:158
  294.4 2.1 constant_dynamic-update-slice_fusion
  296.4 7.2 fusion.98
  303.6 20.2 %convert_reduce_fusion = (f32[768]{0:T(1024)}, bf16[2048,768]{1,0:T(8,128)(2,1)S(1)}, f32[2048,768]{1,0:T(8,128)}) fusion(f32[2048,768]{1,0:T(8,128)} %fusion.98, f32[768]{0:T(1024)} %convert_element_type.159, bf16[2048,768]{1,0:T(8,128)(2,1)} %all-gather.6.cloned.1.call-done, bf16[768,768]{1,0:T(8,128)(2,1)S(1)} %copy-done), kind=kOutput, calls=%fused_computation.64 | convolution fusion | flops 2533883136 | bytes 20060160 | tf_op jit(solution)/shard_map/dot_general | solution.py:198
  325.5 4.0 convolution_convert_fusion
  329.6 5.5 multiply_convert_fusion.1
  336.7 4.0 convolution_convert_fusion.1
  340.8 10.8 %all-gather.8.cloned.1.call-start = ((), (), s32[]{:S(2)}) async-start(), calls=%async_computation.13 | async-start | bytes 3932160 | tf_op jit(solution)/shard_map/all_gather | solution.py:216
  351.6 38.5 %reduce-scatter.15.cloned.1.call-done = bf16[512,768]{1,0:T(8,128)(2,1)} async-done(((bf16[2048,768]{1,0:T(8,128)(2,1)}), bf16[512,768]{1,0:T(8,128)(2,1)}) %reduce-scatter.15.cloned.1.call-update) | async-done | bytes 786448 | tf_op jit(solution)/shard_map/reduce_scatter | solution.py:206
  392.1 2.2 fusion.75
  394.3 58.3 %reduce-scatter.13.cloned.1.call-done = bf16[512,768]{1,0:T(8,128)(2,1)} async-done(((bf16[2048,768]{1,0:T(8,128)(2,1)}), bf16[512,768]{1,0:T(8,128)(2,1)}) %reduce-scatter.13.cloned.1.call-update) | async-done | bytes 786448 | tf_op jit(solution)/shard_map/reduce_scatter | solution.py:172
  452.7 3.4 fusion.94
  458.3 63.4 %all-gather.8.cloned.1.call-done = bf16[2048,768]{1,0:T(8,128)(2,1)} async-done(((bf16[512,768]{1,0:T(8,128)(2,1)}), bf16[2048,768]{1,0:T(8,128)(2,1)}) %all-gather.8.cloned.1.call-update) | async-done | bytes 3145744 | tf_op jit(solution)/shard_map/all_gather | solution.py:216
  521.7 4.1 convolution_bitcast_fusion
  525.9 3.1 convolution_convert_fusion.4
  534.6 31.7 %while.27 = (s32[]{:T(128)}, bf16[4,512,3,64]{1,3,2,0:T(8,128)(2,1)}, bf16[4,512,3,64]{1,3,2,0:T(8,128)(2,1)}, bf16[4,512,3,64]{1,3,2,0:T(8,128)(2,1)}, bf16[4,5...) while((s32[]{:T(128)}, ...), condition=%wide.region_15.16_spmd, body=%wide.region_13.15_spmd.sunk | while | flops 511146496 | bytes 26127476 | solution.py:221
  571.0 2.6 copy.71
  573.6 2.1 stack_reshape.9
  577.7 4.1 convolution_convert_fusion.2
  582.1 7.0 fusion.100
  589.1 6.9 fusion.101
  596.1 6.5 fusion.99
  608.0 33.0 %reduce-scatter.17.cloned.1.call-done = bf16[512,768]{1,0:T(8,128)(2,1)} async-done(((bf16[2048,768]{1,0:T(8,128)(2,1)}), bf16[512,768]{1,0:T(8,128)(2,1)}) %reduce-scatter.17.cloned.1.call-update) | async-done | bytes 786448 | tf_op jit(solution)/shard_map/reduce_scatter | solution.py:245
  642.7 2.1 fusion.76
  644.8 41.8 %all-reduce = (f32[768]{0:T(1024)S(1)}, f32[]{:T(128)}, f32[768]{0:T(1024)S(1)}, f32[768]{0:T(1024)}, f32[768]{0:T(1024)}, /*index=5*/f32[768]{0:T(1024)}, f32[3...) all-reduce(f32[768]{0:T(1024)S(1)} %get-tuple-element.230, ...), channel_id=1, replica_groups=mesh['dp'=8,'tensor'=4] {'dp','tensor'}, use_global_device_ids=true, to_apply=%region_24.25 | all-reduce | flops 10753 | bytes 86024 | tf_op jit(solution)/shard_map/psum | solution.py:182
  687.3 2.6 fusion.78
  690.0 2.6 add_convert_fusion.1
  692.6 41.2 %reduce-scatter.23.cloned.1.call-done = f32[768,96]{0,1:T(8,128)} async-done(((f32[768,768]{0,1:T(8,128)}), f32[768,96]{0,1:T(8,128)}) %reduce-scatter.23.cloned.1.call-update) | async-done | bytes 294928 | tf_op jit(solution)/shard_map/reduce_scatter | solution.py:257
  733.8 44.2 %reduce-scatter.19.cloned.1.call-done = f32[96,576]{1,0:T(8,128)} async-done(((f32[768,576]{1,0:T(8,128)}), f32[96,576]{1,0:T(8,128)}) %reduce-scatter.19.cloned.1.call-update) | async-done | bytes 221200 | tf_op jit(solution)/shard_map/reduce_scatter | solution.py:254
  (236 shorter events, 97.1 us)
Async XLA Ops:
  7.2 296.4 %copy-start = (bf16[768,768]{1,0:T(8,128)(2,1)S(1)}, bf16[768,768]{1,0:T(8,128)(2,1)}, u32[]{:S(2)}) copy-start(bf16[768,768]{1,0:T(8,128)(2,1)} %param.34) | copy-start | bytes 3538948
  7.2 7.4 copy-start.37
  7.2 8.1 %copy-start.38 = (bf16[192]{0:T(256)(128)(2,1)S(1)}, bf16[192]{0:T(256)(128)(2,1)}, u32[]{:S(2)}) copy-start(bf16[192]{0:T(256)(128)(2,1)} %param.26) | copy-start | bytes 1156
  7.2 8.8 %copy-start.22 = (s32[2048]{0:T(1024)S(1)}, s32[2048]{0:T(1024)}, u32[]{:S(2)}) copy-start(s32[2048]{0:T(1024)} %param.21) | copy-start | bytes 24580
  7.2 73.7 %copy-start.41 = (bf16[768,576]{0,1:T(8,128)(2,1)S(1)}, bf16[768,576]{0,1:T(8,128)(2,1)}, u32[]{:S(2)}) copy-start(bf16[768,576]{0,1:T(8,128)(2,1)} %param.25) | copy-start | bytes 2654212
  7.2 73.7 %all-gather.4.cloned.1.call-start = ((), (), s32[]{:S(2)}) async-start(), calls=%async_computation.8 | async-start | bytes 3932160 | tf_op jit(solution)/shard_map/all_gather | solution.py:108
  8.7 76.1 %copy-start.18 = (f32[512]{0:T(512)}, f32[512]{0:T(512)S(1)}, u32[]{:S(2)}) copy-start(f32[512]{0:T(512)S(1)} %broadcast_multiply_fusion.1) | copy-start | bytes 6148
  10.8 74.0 %copy-start.23 = (f32[512]{0:T(512)}, f32[512]{0:T(512)S(1)}, u32[]{:S(2)}) copy-start(f32[512]{0:T(512)S(1)} %fusion.90) | copy-start | bytes 6148
  11.5 73.3 %copy-start.16 = (f32[768]{0:T(1024)}, f32[768]{0:T(1024)S(1)}, u32[]{:S(2)}) copy-start(f32[768]{0:T(1024)S(1)} %convert_element_type.147) | copy-start | bytes 9220
  14.6 168.7 %reduce-scatter.11.cloned.1.call-start = ((), (), s32[]{:S(2)}) async-start(), calls=%async_computation.9 | async-start | bytes 3932160 | tf_op jit(solution)/shard_map/reduce_scatter | solution.py:132
  118.3 5.8 copy-start.6
  118.3 3.1 copy-start.14
  124.1 59.2 %copy-start.2 = (bf16[512,768]{1,0:T(8,128)(2,1)S(1)}, bf16[512,768]{1,0:T(8,128)(2,1)}, u32[]{:S(2)}) copy-start(bf16[512,768]{1,0:T(8,128)(2,1)} %param.20) | copy-start | bytes 2359300
  124.1 179.5 %all-gather.6.cloned.1.call-start = ((), (), s32[]{:S(2)}) async-start(), calls=%async_computation.11 | async-start | bytes 3932160 | tf_op jit(solution)/shard_map/all_gather | solution.py:196
  126.7 263.5 %reduce-scatter.15.cloned.1.call-start = ((), (), s32[]{:S(2)}) async-start(), calls=%async_computation.12 | async-start | bytes 3932160 | tf_op jit(solution)/shard_map/reduce_scatter | solution.py:206
  183.3 5.7 copy-start.3
  183.3 5.7 copy-start.34
  184.9 5.8 copy-start.20
  187.1 3.6 copy-start.25
  190.7 37.8 %collective-permute-start = (bf16[512,768]{1,0:T(8,128)(2,1)}, bf16[512,768]{1,0:T(8,128)(2,1)}, u32[]{:S(2)}, u32[]{:S(2)}) collective-permute-start(bf16[512,768]{1,0:T(8,128)(2,1)} %get-tuple-element.223), channel_id=1, source_target_pairs={{0,1},{1,2},{2,3},{3,0},{4,5},{5,6},{6,7},{7,4},{8,9},{9,10},{10,1... | collective-permute-start | bytes 2359304 | tf_op jit(solution)/shard_map/ppermute | solution.py:158
  191.5 72.2 %collective-permute-start.1 = (bf16[512,768]{1,0:T(8,128)(2,1)}, bf16[512,768]{1,0:T(8,128)(2,1)}, u32[]{:S(2)}, u32[]{:S(2)}) collective-permute-start(bf16[512,768]{1,0:T(8,128)(2,1)} %get-tuple-element.223), channel_id=1, source_target_pairs={{0,3},{1,0},{2,1},{3,2},{4,7},{5,4},{6,5},{7,6},{8,11},{9,8},{10,9... | collective-permute-start | bytes 2359304 | tf_op jit(solution)/shard_map/ppermute | solution.py:163
  228.5 65.9 %collective-permute-start.2 = (bf16[512,768]{1,0:T(8,128)(2,1)}, bf16[512,768]{1,0:T(8,128)(2,1)}, u32[]{:S(2)}, u32[]{:S(2)}) collective-permute-start(bf16[512,768]{1,0:T(8,128)(2,1)} %collective-permute-done), channel_id=1, source_target_pairs={{0,1},{1,2},{2,3},{3,0},{4,5},{5,6},{6,7},{7,4},{8,9},{9,10},{10,1... | collective-permute-start | bytes 2359304 | tf_op jit(solution)/shard_map/ppermute | solution.py:158
  261.6 34.9 %copy-start.39 = (bf16[768,768]{1,0:T(8,128)(2,1)S(1)}, bf16[768,768]{1,0:T(8,128)(2,1)}, u32[]{:S(2)}) copy-start(bf16[768,768]{1,0:T(8,128)(2,1)} %param.32) | copy-start | bytes 3538948
  303.6 21.9 %copy-start.40 = (bf16[768,768]{1,0:T(8,128)(2,1)S(1)}, bf16[768,768]{1,0:T(8,128)(2,1)}, u32[]{:S(2)}) copy-start(bf16[768,768]{1,0:T(8,128)(2,1)} %param.32) | copy-start | bytes 3538948
  329.5 123.1 %reduce-scatter.13.cloned.1.call-start = ((), (), s32[]{:S(2)}) async-start(), calls=%async_computation.10 | async-start | bytes 3932160 | tf_op jit(solution)/shard_map/reduce_scatter | solution.py:172
  340.7 10.9 %copy-start.36 = (bf16[768]{0:T(1024)(128)(2,1)S(1)}, bf16[768]{0:T(1024)(128)(2,1)}, u32[]{:S(2)}) copy-start(bf16[768]{0:T(1024)(128)(2,1)} %param.35) | copy-start | bytes 4612
  340.7 49.4 %copy-start.21 = (f32[512]{0:T(512)S(1)}, f32[512]{0:T(512)}, u32[]{:S(2)}) copy-start(f32[512]{0:T(512)} %copy-done.20) | copy-start | bytes 6148
  340.7 51.4 %copy-start.32 = (f32[512]{0:T(512)S(1)}, f32[512]{0:T(512)}, u32[]{:S(2)}) copy-start(f32[512]{0:T(512)} %copy-done.31) | copy-start | bytes 6148
  340.7 51.4 %copy-start.26 = (f32[512]{0:T(512)S(1)}, f32[512]{0:T(512)}, u32[]{:S(2)}) copy-start(f32[512]{0:T(512)} %copy-done.25) | copy-start | bytes 6148
  340.7 111.9 %copy-start.28 = (f32[512]{0:T(512)S(1)}, f32[512]{0:T(512)}, u32[]{:S(2)}) copy-start(f32[512]{0:T(512)} %copy-done.27) | copy-start | bytes 6148
  340.8 111.9 %copy-start.33 = (f32[512]{0:T(512)S(1)}, f32[512]{0:T(512)}, u32[]{:S(2)}) copy-start(f32[512]{0:T(512)} %get-tuple-element.219) | copy-start | bytes 6148
  340.8 180.9 %all-gather.8.cloned.1.call-start = ((), (), s32[]{:S(2)}) async-start(), calls=%async_computation.13 | async-start | bytes 3932160 | tf_op jit(solution)/shard_map/all_gather | solution.py:216
  390.2 62.5 %copy-start.8 = (bf16[512,768]{1,0:T(8,128)(2,1)S(1)}, bf16[512,768]{1,0:T(8,128)(2,1)}, u32[]{:S(2)}) copy-start(bf16[512,768]{1,0:T(8,128)(2,1)} %reduce-scatter.15.cloned.1.call-done) | copy-start | bytes 2359300
  456.0 65.7 %copy-start.10 = (bf16[24,8,4,512]{3,1,2,0:T(8,128)(2,1)S(1)}, bf16[24,8,4,512]{3,1,2,0:T(8,128)(2,1)}, u32[]{:S(2)}) copy-start(bf16[24,8,4,512]{3,1,2,0:T(8,128)(2,1)} %copy-done.9) | copy-start | bytes 2359300
  458.2 148.2 %reduce-scatter.25.cloned.1.call-start = ((), (), s32[]{:S(2)}) async-start(), calls=%async_computation.18 | async-start | bytes 884736
  458.2 67.6 %copy-start.15 = (bf16[192,768]{1,0:T(8,128)(2,1)S(1)}, bf16[192,768]{1,0:T(8,128)(2,1)}, u32[]{:S(2)}) copy-start(bf16[192,768]{1,0:T(8,128)(2,1)} %param.28) | copy-start | bytes 884740
  525.8 115.1 %reduce-scatter.17.cloned.1.call-start = ((), (), s32[]{:S(2)}) async-start(), calls=%async_computation.14 | async-start | bytes 3932160 | tf_op jit(solution)/shard_map/reduce_scatter | solution.py:245
  529.0 5.6 copy-start.7
  581.8 110.7 %reduce-scatter.21.cloned.1.call-start = ((), (), s32[]{:S(2)}) async-start(), calls=%async_computation.16 | async-start | bytes 2654208 | tf_op jit(solution)/shard_map/reduce_scatter | solution.py:256
  589.1 144.7 %reduce-scatter.23.cloned.1.call-start = ((), (), s32[]{:S(2)}) async-start(), calls=%async_computation.17 | async-start | bytes 2654208 | tf_op jit(solution)/shard_map/reduce_scatter | solution.py:257
  596.1 6.7 copy-start.35
  596.1 181.9 %reduce-scatter.19.cloned.1.call-start = ((), (), s32[]{:S(2)}) async-start(), calls=%async_computation.15 | async-start | bytes 2211840 | tf_op jit(solution)/shard_map/reduce_scatter | solution.py:254
  602.7 38.3 %copy-start.17 = (f32[768]{0:T(1024)S(1)}, f32[768]{0:T(1024)}, u32[]{:S(2)}) copy-start(f32[768]{0:T(1024)} %copy-done.16) | copy-start | bytes 9220
  602.7 38.3 %copy-start.19 = (f32[512]{0:T(512)S(1)}, f32[512]{0:T(512)}, u32[]{:S(2)}) copy-start(f32[512]{0:T(512)} %copy-done.18) | copy-start | bytes 6148
  602.7 40.0 %copy-start.30 = (f32[512]{0:T(512)S(1)}, f32[512]{0:T(512)}, u32[]{:S(2)}) copy-start(f32[512]{0:T(512)} %copy-done.29) | copy-start | bytes 6148
  602.7 40.0 %copy-start.24 = (f32[512]{0:T(512)S(1)}, f32[512]{0:T(512)}, u32[]{:S(2)}) copy-start(f32[512]{0:T(512)} %copy-done.23) | copy-start | bytes 6148
  604.5 85.5 %copy-start.5 = (f32[512,768]{1,0:T(8,128)S(1)}, f32[512,768]{1,0:T(8,128)}, u32[]{:S(2)}) copy-start(f32[512,768]{1,0:T(8,128)} %copy-done.4) | copy-start | bytes 4718596
  687.3 90.7 %copy-start.1 = (bf16[768,768]{1,0:T(8,128)(2,1)S(1)}, bf16[768,768]{1,0:T(8,128)(2,1)}, u32[]{:S(2)}) copy-start(bf16[768,768]{1,0:T(8,128)(2,1)} %param.34) | copy-start | bytes 3538948
  (10 other events, 12.3 us)
Sparse Core Ops, SparseCore 0:
  14.7 66.1 all-gather.3
  124.2 59.0 reduce-scatter.10
  185.5 110.6 all-gather.5
  329.6 60.4 reduce-scatter.14
  392.3 60.3 reduce-scatter.12
  458.3 63.3 all-gather.7
  526.0 33.5 reduce-scatter.24
  581.9 59.0 reduce-scatter.16
  644.9 42.6 reduce-scatter.20
  691.4 42.3 reduce-scatter.22
  737.8 40.1 reduce-scatter.18
